TPU v7x, 32 devices: a whole 2x2x4 slice. The times are simulated.
32 devices in a mesh: py: 8 (over z, x), px: 4 (over y, core).
Axes of the slice: x: 2, y: 2, z: 4, core: 2. Of those that a mesh axis runs over, the one named last changes fastest.
Arguments:
- density: float32 [256, 128, 128], P('py', 'px'), may hold values from 0.5 to 2
- conductance: float32 [256, 128, 128], P('py', 'px'), may hold values from 0.03 to 0.22
- source: float32 [256, 128, 128], P('py', 'px'), may hold values from -0.2 to 0.2
Outputs:
- anomaly: float32 [256, 128, 128], P('py', 'px')
- density_end: float32 [256, 128, 128], P('py', 'px')
All inputs are finite; a program needn't handle non-finite values.
Results may differ from a plain program's by a relative error of at most 0.00002.
Values sent between devices are 32-bit elements; how exact they have to be, the bound alone decides.
A program may use at most 64 MiB of HBM per device.

v0:
```python
import jax
import jax.numpy as jnp
from jax import lax
from jax.sharding import PartitionSpec as P

STEPS = 6


def with_halo(cells, sides, width):
    for axis, dim in sides:
        count = lax.axis_size(axis)
        ends = count - 1
        head = lax.slice_in_dim(cells, 0, width, axis=dim)
        tail = lax.slice_in_dim(cells, cells.shape[dim] - width, cells.shape[dim], axis=dim)
        cells = jnp.concatenate(
            [
                lax.ppermute(tail, axis, [(i, (i + 1) % count) for i in range(ends)]),
                cells,
                lax.ppermute(head, axis, [((i + 1) % count, i) for i in range(ends)]),
            ],
            axis=dim,
        )
    return cells


def strip_edges(values, dims):
    for dim in dims:
        values = lax.slice_in_dim(values, 1, values.shape[dim] - 1, axis=dim)
    return values


def neighbour(values, dim, start, dims):
    others = [other for other in dims if other != dim]
    values = strip_edges(values, others)
    return lax.slice_in_dim(values, start, start + values.shape[dim] - 2, axis=dim)


def one_step(padded, conductance, source):
    middle = strip_edges(padded, (0, 1))
    lower = [neighbour(padded, dim, 0, (0, 1)) for dim in (0, 1)]
    upper = [neighbour(padded, dim, 2, (0, 1)) for dim in (0, 1)]
    spread = lower[0] + upper[0] + lower[1] + upper[1] - 4.0 * middle
    return middle + conductance * spread + source


def per_device(density, conductance, source):
    padded = with_halo(density, (("py", 0), ("px", 1)), STEPS)
    wide_parts = with_halo(
        jnp.concatenate([conductance, source], axis=2), (("py", 0), ("px", 1)), STEPS - 1
    )
    wide_conductance, wide_source = jnp.split(wide_parts, 2, axis=2)
    for step in range(STEPS):
        later = one_step(padded, wide_conductance, wide_source)
        values = later
        margin = STEPS - 1 - step
        place = lax.axis_index("py") * density.shape[0] - margin + jnp.arange(values.shape[0])
        keep_cells = (place >= 0) & (place < density.shape[0] * lax.axis_size("py"))
        values = jnp.where(keep_cells.reshape((-1,) + (1,) * 2), values, 0.0)
        place = lax.axis_index("px") * density.shape[1] - margin + jnp.arange(values.shape[1])
        keep_cells = (place >= 0) & (place < density.shape[1] * lax.axis_size("px"))
        values = jnp.where(keep_cells.reshape((-1,) + (1,) * 1), values, 0.0)
        later = values
        if step < STEPS - 1:
            wide_conductance = strip_edges(wide_conductance, (0, 1))
            wide_source = strip_edges(wide_source, (0, 1))
        padded = later
    density = padded
    count = density.shape[0] * lax.axis_size("py")
    line_mean = lax.psum(jnp.sum(density, axis=0, keepdims=True), "py") / count
    centred = density - line_mean
    line_variance = lax.psum(jnp.sum(centred * centred, axis=0, keepdims=True), "py") / count
    anomaly = centred * lax.rsqrt(line_variance + 0.0001)
    return (anomaly, density)


def solution(mesh):
    in_specs = (P("py", "px", None), P("py", "px", None), P("py", "px", None))
    out_specs = (P("py", "px", None), P("py", "px", None))
    return jax.shard_map(
        per_device, mesh=mesh, in_specs=in_specs, out_specs=out_specs, check_vma=False
    )
```

profile of v0, /device:TPU:4, one launch (start us, length us, event | category | flops | bytes accessed | tf_op | source)
XLA Modules:
  0.0 108.5 jit_solution(7742609945512522112)
XLA Ops:
  0.6 0.0 copy-start.3
  0.6 1.1 %constant_dynamic-update-slice_fusion.4 = f32[32,32,256]{2,1,0:T(8,128)S(1)} fusion(f32[32,32,128]{2,1,0:T(8,128)} %param.4), kind=kLoop, calls=%fused_computation.67 | loop fusion | bytes 1048576
  1.8 1.1 constant_dynamic-update-slice_fusion.3
  2.9 1.3 %collective-permute-start.5 = (f32[5,32,256]{2,1,0:T(8,128)S(1)}, f32[5,32,256]{2,1,0:T(8,128)S(1)}, u32[]{:S(2)}, u32[]{:S(2)}) collective-permute-start(f32[5,32,256]{2,1,0:T(8,128)S(1)} %get-tuple-element.7), channel_id=1, source_target_pairs={{4,0},{8,4},{12,8},{16,12},{20,16},{24,20},{28,24},{5,1},{9,5},{13... | collective-permute-start | bytes 491528 | tf_op jit(solution)/shard_map/ppermute | solution.py:19
  4.2 4.6 %collective-permute-start.4 = (f32[5,32,256]{2,1,0:T(8,128)S(1)}, f32[5,32,256]{2,1,0:T(8,128)S(1)}, u32[]{:S(2)}, u32[]{:S(2)}) collective-permute-start(f32[5,32,256]{2,1,0:T(8,128)S(1)} %get-tuple-element.6), channel_id=1, source_target_pairs={{0,4},{4,8},{8,12},{12,16},{16,20},{20,24},{24,28},{1,5},{5,9},{9,... | collective-permute-start | bytes 491528 | tf_op jit(solution)/shard_map/ppermute | solution.py:17
  8.8 0.0 copy-done.3
  8.8 4.3 %collective-permute-start = (f32[6,32,128]{2,1,0:T(8,128)S(1)}, f32[6,32,128]{2,1,0:T(8,128)S(1)}, u32[]{:S(2)}, u32[]{:S(2)}) collective-permute-start(f32[6,32,128]{2,1,0:T(8,128)S(1)} %get-tuple-element.11), channel_id=1, source_target_pairs={{0,4},{4,8},{8,12},{12,16},{16,20},{20,24},{24,28},{1,5},{5,9},{9,... | collective-permute-start | bytes 294920 | tf_op jit(solution)/shard_map/ppermute | solution.py:17
  13.1 1.3 %collective-permute-start.1 = (f32[6,32,128]{2,1,0:T(8,128)S(1)}, f32[6,32,128]{2,1,0:T(8,128)S(1)}, u32[]{:S(2)}, u32[]{:S(2)}) collective-permute-start(f32[6,32,128]{2,1,0:T(8,128)S(1)} %get-tuple-element.10), channel_id=1, source_target_pairs={{4,0},{8,4},{12,8},{16,12},{20,16},{24,20},{28,24},{5,1},{9,5},{13... | collective-permute-start | bytes 294920 | tf_op jit(solution)/shard_map/ppermute | solution.py:19
  14.5 2.9 %collective-permute-done = f32[6,32,128]{2,1,0:T(8,128)S(1)} collective-permute-done((f32[6,32,128]{2,1,0:T(8,128)S(1)}, f32[6,32,128]{2,1,0:T(8,128)S(1)}, u32[]{:S(2)}, u32[]{:S(2)}) %collective-permute-start) | collective-permute-done | bytes 98336 | tf_op jit(solution)/shard_map/ppermute | solution.py:17
  17.4 2.2 %collective-permute-done.1 = f32[6,32,128]{2,1,0:T(8,128)S(1)} collective-permute-done((f32[6,32,128]{2,1,0:T(8,128)S(1)}, f32[6,32,128]{2,1,0:T(8,128)S(1)}, u32[]{:S(2)}, u32[]{:S(2)}) %collective-permute-start.1) | collective-permute-done | bytes 98336 | tf_op jit(solution)/shard_map/ppermute | solution.py:19
  19.7 1.9 %collective-permute-start.3 = (f32[44,6,128]{2,1,0:T(8,128)S(1)}, f32[44,6,128]{2,1,0:T(8,128)S(1)}, u32[]{:S(2)}, u32[]{:S(2)}) collective-permute-start(f32[44,6,128]{2,1,0:T(8,128)S(1)} %get-tuple-element.9), channel_id=1, source_target_pairs={{1,0},{2,1},{3,2},{5,4},{6,5},{7,6},{9,8},{10,9},{11,10},{13,12},{... | collective-permute-start | bytes 405512 | tf_op jit(solution)/shard_map/ppermute | solution.py:19
  21.6 2.4 %collective-permute-start.2 = (f32[44,6,128]{2,1,0:T(8,128)S(1)}, f32[44,6,128]{2,1,0:T(8,128)S(1)}, u32[]{:S(2)}, u32[]{:S(2)}) collective-permute-start(f32[44,6,128]{2,1,0:T(8,128)S(1)} %get-tuple-element.8), channel_id=1, source_target_pairs={{0,1},{1,2},{2,3},{4,5},{5,6},{6,7},{8,9},{9,10},{10,11},{12,13},{... | collective-permute-start | bytes 405512 | tf_op jit(solution)/shard_map/ppermute | solution.py:17
  24.0 0.0 collective-permute-done.5
  24.0 0.0 collective-permute-done.4
  24.0 0.1 pad_maximum_fusion.4
  24.1 3.1 %collective-permute-start.7 = (f32[42,5,256]{2,1,0:T(8,128)S(1)}, f32[42,5,256]{2,1,0:T(8,128)S(1)}, u32[]{:S(2)}, u32[]{:S(2)}) collective-permute-start(f32[42,5,256]{2,1,0:T(8,128)S(1)} %get-tuple-element.5), channel_id=1, source_target_pairs={{1,0},{2,1},{3,2},{5,4},{6,5},{7,6},{9,8},{10,9},{11,10},{13,12},{... | collective-permute-start | bytes 645128 | tf_op jit(solution)/shard_map/ppermute | solution.py:19
  27.3 1.9 %collective-permute-start.6 = (f32[42,5,256]{2,1,0:T(8,128)S(1)}, f32[42,5,256]{2,1,0:T(8,128)S(1)}, u32[]{:S(2)}, u32[]{:S(2)}) collective-permute-start(f32[42,5,256]{2,1,0:T(8,128)S(1)} %get-tuple-element.4), channel_id=1, source_target_pairs={{0,1},{1,2},{2,3},{4,5},{5,6},{6,7},{8,9},{9,10},{10,11},{12,13},{... | collective-permute-start | bytes 645128 | tf_op jit(solution)/shard_map/ppermute | solution.py:17
  29.2 0.0 collective-permute-done.3
  29.2 0.0 collective-permute-done.2
  29.2 0.1 pad_maximum_fusion.1
  29.4 2.6 %collective-permute-done.7 = f32[42,5,256]{2,1,0:T(8,128)S(1)} collective-permute-done((f32[42,5,256]{2,1,0:T(8,128)S(1)}, f32[42,5,256]{2,1,0:T(8,128)S(1)}, u32[]{:S(2)}, u32[]{:S(2)}) %collective-permute-start.7) | collective-permute-done | bytes 215072 | tf_op jit(solution)/shard_map/ppermute | solution.py:19
  32.0 3.8 %collective-permute-done.6 = f32[42,5,256]{2,1,0:T(8,128)S(1)} collective-permute-done((f32[42,5,256]{2,1,0:T(8,128)S(1)}, f32[42,5,256]{2,1,0:T(8,128)S(1)}, u32[]{:S(2)}, u32[]{:S(2)}) %collective-permute-start.6) | collective-permute-done | bytes 215072 | tf_op jit(solution)/shard_map/ppermute | solution.py:17
  35.8 0.3 pad_maximum_fusion
  36.1 0.5 fusion.1
  36.7 0.5 fusion.6
  37.2 0.5 fusion.11
  37.7 0.5 fusion.16
  38.2 0.0 copy-start.1
  38.3 0.0 copy-start.2
  38.3 0.5 fusion.21
  38.7 0.5 copy-done.1
  39.3 0.2 copy-done.2
  39.4 0.3 fusion.31
  39.7 0.0 copy-start
  39.7 34.8 %psum.14 = f32[1,32,128]{2,1,0:T(8,128)S(1)} all-reduce(f32[1,32,128]{2,1,0:T(8,128)S(1)} %bitcast.6), channel_id=1, replica_groups=mesh['py'=8,'px'=4] {'py'}, use_global_device_ids=true, to_apply=%region_1.2 | all-reduce | flops 4096 | bytes 32768 | tf_op jit(solution)/shard_map/psum | solution.py:69
  74.5 0.1 multiply_reduce_fusion
  74.6 33.0 %psum.15 = f32[1,32,128]{2,1,0:T(8,128)S(1)} all-reduce(f32[1,32,128]{2,1,0:T(8,128)S(1)} %bitcast.7), channel_id=1, replica_groups=mesh['py'=8,'px'=4] {'py'}, use_global_device_ids=true, to_apply=%region_3.4 | all-reduce | flops 4096 | bytes 32768 | tf_op jit(solution)/shard_map/psum | solution.py:71
  107.6 0.9 subtract_multiply_fusion
  108.5 0.0 copy-done
  (14 shorter events, 0.2 us)
Async XLA Ops:
  0.6 8.1 %copy-start.3 = (f32[32,32,128]{2,1,0:T(8,128)S(1)}, f32[32,32,128]{2,1,0:T(8,128)}, u32[]{:S(2)}) copy-start(f32[32,32,128]{2,1,0:T(8,128)} %param.3) | copy-start | bytes 1572868
  2.9 21.1 %collective-permute-start.5 = (f32[5,32,256]{2,1,0:T(8,128)S(1)}, f32[5,32,256]{2,1,0:T(8,128)S(1)}, u32[]{:S(2)}, u32[]{:S(2)}) collective-permute-start(f32[5,32,256]{2,1,0:T(8,128)S(1)} %get-tuple-element.7), channel_id=1, source_target_pairs={{4,0},{8,4},{12,8},{16,12},{20,16},{24,20},{28,24},{5,1},{9,5},{13... | collective-permute-start | bytes 491528 | tf_op jit(solution)/shard_map/ppermute | solution.py:19
  4.2 19.8 %collective-permute-start.4 = (f32[5,32,256]{2,1,0:T(8,128)S(1)}, f32[5,32,256]{2,1,0:T(8,128)S(1)}, u32[]{:S(2)}, u32[]{:S(2)}) collective-permute-start(f32[5,32,256]{2,1,0:T(8,128)S(1)} %get-tuple-element.6), channel_id=1, source_target_pairs={{0,4},{4,8},{8,12},{12,16},{16,20},{20,24},{24,28},{1,5},{5,9},{9,... | collective-permute-start | bytes 491528 | tf_op jit(solution)/shard_map/ppermute | solution.py:17
  8.8 8.5 %collective-permute-start = (f32[6,32,128]{2,1,0:T(8,128)S(1)}, f32[6,32,128]{2,1,0:T(8,128)S(1)}, u32[]{:S(2)}, u32[]{:S(2)}) collective-permute-start(f32[6,32,128]{2,1,0:T(8,128)S(1)} %get-tuple-element.11), channel_id=1, source_target_pairs={{0,4},{4,8},{8,12},{12,16},{16,20},{20,24},{24,28},{1,5},{5,9},{9,... | collective-permute-start | bytes 294920 | tf_op jit(solution)/shard_map/ppermute | solution.py:17
  13.1 6.5 %collective-permute-start.1 = (f32[6,32,128]{2,1,0:T(8,128)S(1)}, f32[6,32,128]{2,1,0:T(8,128)S(1)}, u32[]{:S(2)}, u32[]{:S(2)}) collective-permute-start(f32[6,32,128]{2,1,0:T(8,128)S(1)} %get-tuple-element.10), channel_id=1, source_target_pairs={{4,0},{8,4},{12,8},{16,12},{20,16},{24,20},{28,24},{5,1},{9,5},{13... | collective-permute-start | bytes 294920 | tf_op jit(solution)/shard_map/ppermute | solution.py:19
  19.7 9.5 %collective-permute-start.3 = (f32[44,6,128]{2,1,0:T(8,128)S(1)}, f32[44,6,128]{2,1,0:T(8,128)S(1)}, u32[]{:S(2)}, u32[]{:S(2)}) collective-permute-start(f32[44,6,128]{2,1,0:T(8,128)S(1)} %get-tuple-element.9), channel_id=1, source_target_pairs={{1,0},{2,1},{3,2},{5,4},{6,5},{7,6},{9,8},{10,9},{11,10},{13,12},{... | collective-permute-start | bytes 405512 | tf_op jit(solution)/shard_map/ppermute | solution.py:19
  21.6 7.6 %collective-permute-start.2 = (f32[44,6,128]{2,1,0:T(8,128)S(1)}, f32[44,6,128]{2,1,0:T(8,128)S(1)}, u32[]{:S(2)}, u32[]{:S(2)}) collective-permute-start(f32[44,6,128]{2,1,0:T(8,128)S(1)} %get-tuple-element.8), channel_id=1, source_target_pairs={{0,1},{1,2},{2,3},{4,5},{5,6},{6,7},{8,9},{9,10},{10,11},{12,13},{... | collective-permute-start | bytes 405512 | tf_op jit(solution)/shard_map/ppermute | solution.py:17
  24.1 7.9 %collective-permute-start.7 = (f32[42,5,256]{2,1,0:T(8,128)S(1)}, f32[42,5,256]{2,1,0:T(8,128)S(1)}, u32[]{:S(2)}, u32[]{:S(2)}) collective-permute-start(f32[42,5,256]{2,1,0:T(8,128)S(1)} %get-tuple-element.5), channel_id=1, source_target_pairs={{1,0},{2,1},{3,2},{5,4},{6,5},{7,6},{9,8},{10,9},{11,10},{13,12},{... | collective-permute-start | bytes 645128 | tf_op jit(solution)/shard_map/ppermute | solution.py:19
  27.3 8.6 %collective-permute-start.6 = (f32[42,5,256]{2,1,0:T(8,128)S(1)}, f32[42,5,256]{2,1,0:T(8,128)S(1)}, u32[]{:S(2)}, u32[]{:S(2)}) collective-permute-start(f32[42,5,256]{2,1,0:T(8,128)S(1)} %get-tuple-element.4), channel_id=1, source_target_pairs={{0,1},{1,2},{2,3},{4,5},{5,6},{6,7},{8,9},{9,10},{10,11},{12,13},{... | collective-permute-start | bytes 645128 | tf_op jit(solution)/shard_map/ppermute | solution.py:17
  38.2 1.0 copy-start.1
  38.3 1.2 %copy-start.2 = (f32[32,32,128]{2,1,0:T(8,128)S(1)}, f32[32,32,128]{2,1,0:T(8,128)}, u32[]{:S(2)}) copy-start(f32[32,32,128]{2,1,0:T(8,128)} %param.4) | copy-start | bytes 1572868
  39.7 68.7 %copy-start = (f32[32,32,128]{2,1,0:T(8,128)}, f32[32,32,128]{2,1,0:T(8,128)S(1)}, u32[]{:S(2)}) copy-start(f32[32,32,128]{2,1,0:T(8,128)S(1)} %get-tuple-element.3) | copy-start | bytes 1572868
where the time goes:
time: 109 us; the launch traced here: 108 us
  blocking collectives  67.8 us (62%)
  starting transfers between devices  20.8 us (19%)
  waiting for transfers between devices  11.5 us (11%)
  other arithmetic  4.37 us (4%)
  local copies, waits for them, and re-layouts  3.05 us (3%)
    psum x1, blocking collectives, per_device(): line_mean = lax.psum(jnp.sum(density, axis=0, keepdims=True), 'py') / count  34.8 us
    psum x1, blocking collectives, per_device(): lax.psum(jnp.sum(centred * centred, axis=0, keepdims=True), 'py') / count  33 us
    ppermute x4, starting transfers between devices, with_halo(): lax.ppermute(tail, axis, [(i, (i + 1) % count) for i in range(ends)])  13.2 us
    ppermute x4, starting transfers between devices, with_halo(): lax.ppermute(head, axis, [((i + 1) % count, i) for i in range(ends)])  7.65 us
    ppermute x4, waiting for transfers between devices, with_halo(): lax.ppermute(tail, axis, [(i, (i + 1) % count) for i in range(ends)])  6.68 us
    ppermute x4, waiting for transfers between devices, with_halo(): lax.ppermute(head, axis, [((i + 1) % count, i) for i in range(ends)])  4.86 us
    select_n x5, other arithmetic, per_device(): values = jnp.where(keep_cells.reshape((-1,) + (1,) * 1), values, 0.0)  2.55 us
  transfers between devices with their start and end apart: 8, of which 4 were waited for; matrix products, arithmetic and copies ran while one was open for 0% of the time, Pallas kernels for 0%

commit v1 on v0

v1 whole, which is shorter than its diff:
```python
import functools

import jax
import jax.numpy as jnp
from jax import lax
from jax.experimental import pallas as pl
from jax.experimental.pallas import tpu as pltpu
from jax.sharding import PartitionSpec as P

ROUNDS = (3, 3)
DEEP = max(ROUNDS)
PAD = 4
DIRECTIONS = [(0, -1), (0, 1), (-1, 0), (1, 0), (-1, -1), (-1, 1), (1, -1), (1, 1)]
MESH = pl.DeviceIdType.MESH


def edge(direction, size, depth, own):
    if direction < 0:
        return (own, depth), (own + size, depth)
    if direction > 0:
        return (own + size - depth, depth), (own - depth, depth)
    return (own, size), (own, size)


def kernel(py, px, field, conductance, source, density_out, mean_out, scale_out,
           padded, work, coefficients, stats, local_sem, send_sem, recv_sem, stat_send, stat_recv):
    rows, columns, levels = field.shape
    width = columns + 2 * PAD
    my, mx = lax.axis_index("py"), lax.axis_index("px")

    def exists(dy, dx):
        here = jnp.bool_(True)
        if dy:
            here = here & ((my > 0) if dy < 0 else (my < py - 1))
        if dx:
            here = here & ((mx > 0) if dx < 0 else (mx < px - 1))
        return here

    inner = (pl.ds(DEEP, rows), pl.ds(PAD, columns))
    loads = []
    for i, (src, dst) in enumerate(
        [(field, padded.at[0]), (conductance, coefficients.at[0]), (source, coefficients.at[1])]
    ):
        loads.append(pltpu.make_async_copy(src, dst.at[inner], local_sem.at[i]))
        loads[-1].start()

    barrier = pltpu.get_barrier_semaphore()
    expected = jnp.int32(py - 1)
    for step in range(1, py):
        pl.semaphore_signal(barrier, 1, device_id=(lax.rem(my + step, py), mx), device_id_type=MESH)
    for dy, dx in DIRECTIONS:
        if dx:
            there = exists(dy, dx)
            expected = expected + there.astype(jnp.int32)

            @pl.when(there)
            def _():
                pl.semaphore_signal(barrier, 1, device_id=(my + dy, mx + dx), device_id_type=MESH)

    holders = [padded.at[r] for r in range(len(ROUNDS))] + [coefficients.at[0], coefficients.at[1]]
    for dim, direction in ((0, -1), (0, 1), (1, -1), (1, 1)):
        outside = ~exists(*((direction, 0) if dim == 0 else (0, direction)))

        @pl.when(outside)
        def _():
            for holder in holders:
                if dim == 0:
                    start = 0 if direction < 0 else DEEP + rows
                    holder[pl.ds(start, DEEP)] = jnp.zeros((DEEP, width, levels), jnp.float32)
                else:
                    start = 0 if direction < 0 else PAD + columns
                    holder[:, pl.ds(start, PAD)] = jnp.zeros((rows + 2 * DEEP, PAD, levels), jnp.float32)

    pl.semaphore_wait(barrier, expected)

    def exchange(number, arrays):
        for d, (dy, dx) in enumerate(DIRECTIONS):
            copies = []
            for a, (src, row0, column0, dst, depth) in enumerate(arrays):
                reach = depth - 1 if dy and dx else depth
                if reach < 1:
                    continue
                (y_from, y_size), _ = edge(dy, rows, reach, row0)
                (x_from, x_size), _ = edge(dx, columns, reach, column0)
                _, (y_to, _) = edge(dy, rows, reach, DEEP)
                _, (x_to, _) = edge(dx, columns, reach, PAD)
                copies.append(
                    pltpu.make_async_remote_copy(
                        src_ref=src.at[pl.ds(y_from, y_size), pl.ds(x_from, x_size)],
                        dst_ref=dst.at[pl.ds(y_to, y_size), pl.ds(x_to, x_size)],
                        send_sem=send_sem.at[number, a, d],
                        recv_sem=recv_sem.at[number, a, d],
                        device_id=(my + dy, mx + dx),
                        device_id_type=MESH,
                    )
                )
            yield (dy, dx), copies

    def start(copies):
        for (dy, dx), group in copies:
            @pl.when(exists(dy, dx))
            def _():
                for copy in group:
                    copy.start()

    def wait_recv(copies):
        for (dy, dx), group in copies:
            @pl.when(exists(-dy, -dx))
            def _():
                for copy in group:
                    copy.wait_recv()

    def wait_send(copies):
        for (dy, dx), group in copies:
            @pl.when(exists(dy, dx))
            def _():
                for copy in group:
                    copy.wait_send()

    tall = rows + 2 * DEEP
    flat_conductance = coefficients.at[0].reshape(tall * width, levels)
    flat_source = coefficients.at[1].reshape(tall * width, levels)

    def advance(old, first, count, column, wide, put, carry):
        flat = old.reshape(tall * width, levels)

        def row(i, state):
            above, middle, carry = state
            at = (first + i) * width + column
            below = flat[pl.ds(at + width, wide), :]
            sides = flat[pl.ds(at - 1, wide), :] + flat[pl.ds(at + 1, wide), :]
            spread = (above + below) + sides - 4.0 * middle
            later = middle + flat_conductance[pl.ds(at, wide), :] * spread + flat_source[pl.ds(at, wide), :]
            return middle, below, put(i, later, carry)

        at = first * width + column
        state = (flat[pl.ds(at - width, wide), :], flat[pl.ds(at, wide), :], carry)
        return lax.fori_loop(0, count, row, state, unroll=2)[2]

    total = jnp.zeros((columns, levels), jnp.float32)
    waiting = []
    for number, steps in enumerate(ROUNDS):
        if number == 0:
            arrays = [
                (field, 0, 0, padded.at[0], steps),
                (conductance, 0, 0, coefficients.at[0], DEEP - 1),
                (source, 0, 0, coefficients.at[1], DEEP - 1),
            ]
        else:
            arrays = [(padded.at[number], DEEP, PAD, padded.at[number], steps)]
        copies = list(exchange(number, arrays))
        start(copies)
        if number == 0:
            for copy in loads:
                copy.wait()
        wait_recv(copies)
        waiting.append(copies)
        old = padded.at[number]
        for step in range(steps):
            margin = steps - 1 - step
            if margin:
                new = work.at[step % 2]
                flat_new = new.reshape(tall * width, levels)
                first = DEEP - margin

                def put(i, later, carry, first=first, flat_new=flat_new):
                    flat_new[pl.ds((first + i) * width, width), :] = later
                    return carry

                advance(old, first, rows + 2 * margin, 0, width, put, 0)
                old = new
            elif number < len(ROUNDS) - 1:
                flat_new = padded.at[number + 1].reshape(tall * width, levels)

                def put(i, later, carry, flat_new=flat_new):
                    flat_new[pl.ds((DEEP + i) * width + PAD, columns), :] = later
                    return carry

                advance(old, DEEP, rows, PAD, columns, put, 0)
            else:

                def put(i, later, carry):
                    density_out[i] = later
                    return carry + later

                total = advance(old, DEEP, rows, PAD, columns, put, total)

    local_mean = total * (1.0 / rows)

    def square(i, carry):
        away = density_out[i] - local_mean
        return carry + away * away

    squares = lax.fori_loop(0, rows, square, jnp.zeros((columns, levels), jnp.float32), unroll=4)
    stats[0, 0] = local_mean
    stats[0, 1] = squares
    order = sorted(range(1, py), key=lambda step: -min(step, py - step))
    sums = []
    for step in order:
        copy = pltpu.make_async_remote_copy(
            src_ref=stats.at[0],
            dst_ref=stats.at[step],
            send_sem=stat_send.at[step],
            recv_sem=stat_recv.at[step],
            device_id=(lax.rem(my + step, py), mx),
            device_id_type=MESH,
        )
        copy.start()
        sums.append(copy)
    for copies in waiting:
        wait_send(copies)
    for copy in sums:
        copy.wait_recv()
    mean = stats[0, 0]
    for step in range(1, py):
        mean = mean + stats[step, 0]
    mean = mean * (1.0 / py)
    inside = stats[0, 1]
    between = (stats[0, 0] - mean) * (stats[0, 0] - mean)
    for step in range(1, py):
        inside = inside + stats[step, 1]
        between = between + (stats[step, 0] - mean) * (stats[step, 0] - mean)
    variance = inside * (1.0 / (rows * py)) + between * (1.0 / py)
    mean_out[...] = mean
    scale_out[...] = lax.rsqrt(variance + 0.0001)
    for copy in sums:
        copy.wait_send()


def per_device(py, px, density, conductance, source):
    rows, columns, levels = density.shape
    tall, width = rows + 2 * DEEP, columns + 2 * PAD
    vmem = pl.BlockSpec(memory_space=pltpu.VMEM)
    line = jax.ShapeDtypeStruct((columns, levels), jnp.float32)
    density, mean, scale = pl.pallas_call(
        functools.partial(kernel, py, px),
        out_shape=[jax.ShapeDtypeStruct(density.shape, jnp.float32), line, line],
        in_specs=[pl.BlockSpec(memory_space=pl.ANY)] * 3,
        out_specs=[vmem] * 3,
        scratch_shapes=[
            pltpu.VMEM((len(ROUNDS), tall, width, levels), jnp.float32),
            pltpu.VMEM((2, tall, width, levels), jnp.float32),
            pltpu.VMEM((2, tall, width, levels), jnp.float32),
            pltpu.VMEM((py, 2, columns, levels), jnp.float32),
            pltpu.SemaphoreType.DMA((3,)),
            pltpu.SemaphoreType.DMA((len(ROUNDS), 3, len(DIRECTIONS))),
            pltpu.SemaphoreType.DMA((len(ROUNDS), 3, len(DIRECTIONS))),
            pltpu.SemaphoreType.DMA((py,)),
            pltpu.SemaphoreType.DMA((py,)),
        ],
        compiler_params=pltpu.CompilerParams(collective_id=0, has_side_effects=True),
    )(density, conductance, source)
    return (density - mean) * scale, density


def solution(mesh):
    spec = P("py", "px", None)
    return jax.shard_map(
        functools.partial(per_device, mesh.shape["py"], mesh.shape["px"]),
        mesh=mesh, in_specs=(spec,) * 3, out_specs=(spec,) * 2, check_vma=False,
    )
```

time: 109 us -> 30.8 us (0.28)
  the two profiles are of different devices: /device:TPU:4 before, /device:TPU:0 now
where the time goes in v1:
time: 30.8 us; the launch traced here: 30.6 us
  Pallas kernels  27.2 us (88%)
  other arithmetic  1.98 us (6%)
  local copies, waits for them, and re-layouts  0.8 us (3%)
  between operations  0.65 us (2%)
    pallas_call x1, Pallas kernels, per_device(): pl.pallas_call(functools.partial(kernel, py, px), out_shape=[jax.ShapeDty...  27.2 us
    mul x1, other arithmetic, per_device(): return ((density - mean) * scale, density)  1.98 us
    unnamed x3, local copies, waits for them, and re-layouts  0.8 us

profile of v1, /device:TPU:0, one launch (start us, length us, event | category | flops | bytes accessed | tf_op | source)
XLA Modules:
  0.0 30.6 jit_solution(8494729137953040301)
XLA Ops:
  0.6 27.2 %shard_map.50 = (f32[32,32,128]{2,1,0:T(8,128)}, f32[32,128]{1,0:T(8,128)}, f32[32,128]{1,0:T(8,128)}) custom-call(f32[32,32,128]{2,1,0:T(8,128)} %field.1, f32[32,32,128]{2,1,0:T(8,128)} %conductance.1, f32[32,32,128]{2,1,0:T(8,128)} %source.1), custom_call_target="tpu_custom_call" | custom-call | tf_op jit(solution)/shard_map/pallas_call | solution.py:235
  27.8 0.0 copy-start
  27.8 2.0 %subtract_multiply_fusion = f32[32,32,128]{2,1,0:T(8,128)} fusion(f32[32,32,128]{2,1,0:T(8,128)} %get-tuple-element.11, f32[32,128]{1,0:T(8,128)} %get-tuple-element.7, f32[32,128]{1,0:T(8,128)} %get-tuple-element.6), kind=kLoop, calls=%fused_computation | loop fusion | flops 262144 | bytes 1081344 | tf_op jit(solution)/shard_map/mul | solution.py:253
  29.8 0.0 copy-done
  29.8 0.8 %copy.6 = f32[32,32,128]{2,1,0:T(8,128)} copy(f32[32,32,128]{2,1,0:T(8,128)S(1)} %copy-done) | data formatting | bytes 1048576
Async XLA Ops:
  27.8 2.0 %copy-start = (f32[32,32,128]{2,1,0:T(8,128)S(1)}, f32[32,32,128]{2,1,0:T(8,128)}, u32[]{:S(2)}) copy-start(f32[32,32,128]{2,1,0:T(8,128)} %get-tuple-element.11) | copy-start | bytes 1572868

commit v2 on v1

--- a/solution.py
+++ b/solution.py
@@ -142,17 +142,17 @@
     for number, steps in enumerate(ROUNDS):
         if number == 0:
             arrays = [
-                (field, 0, 0, padded.at[0], steps),
-                (conductance, 0, 0, coefficients.at[0], DEEP - 1),
-                (source, 0, 0, coefficients.at[1], DEEP - 1),
+                (padded.at[0], DEEP, PAD, padded.at[0], steps),
+                (coefficients.at[0], DEEP, PAD, coefficients.at[0], DEEP - 1),
+                (coefficients.at[1], DEEP, PAD, coefficients.at[1], DEEP - 1),
             ]
         else:
             arrays = [(padded.at[number], DEEP, PAD, padded.at[number], steps)]
         copies = list(exchange(number, arrays))
-        start(copies)
         if number == 0:
             for copy in loads:
                 copy.wait()
+        start(copies)
         wait_recv(copies)
         waiting.append(copies)
         old = padded.at[number]
@@ -226,16 +226,36 @@
     for copy in sums:
         copy.wait_send()
 
+CHUNKS = 4
+
+
+def finish(density, mean, scale, anomaly_out, density_out, anomaly, sem):
+    rows = density.shape[0]
+    whole = pltpu.make_async_copy(density, density_out, sem.at[CHUNKS])
+    whole.start()
+    part = rows // CHUNKS
+    copies = []
+    for chunk in range(CHUNKS):
+        for i in range(chunk * part, (chunk + 1) * part):
+            anomaly[i] = (density[i] - mean[...]) * scale[...]
+        own = pl.ds(chunk * part, part)
+        copies.append(pltpu.make_async_copy(anomaly.at[own], anomaly_out.at[own], sem.at[chunk]))
+        copies[-1].start()
+    for copy in copies:
+        copy.wait()
+    whole.wait()
+
 
 def per_device(py, px, density, conductance, source):
     rows, columns, levels = density.shape
     tall, width = rows + 2 * DEEP, columns + 2 * PAD
     vmem = pl.BlockSpec(memory_space=pltpu.VMEM)
     line = jax.ShapeDtypeStruct((columns, levels), jnp.float32)
+    density, conductance, source = (pltpu.with_memory_space_constraint(x, pltpu.HBM) for x in (density, conductance, source))
     density, mean, scale = pl.pallas_call(
         functools.partial(kernel, py, px),
         out_shape=[jax.ShapeDtypeStruct(density.shape, jnp.float32), line, line],
-        in_specs=[pl.BlockSpec(memory_space=pl.ANY)] * 3,
+        in_specs=[pl.BlockSpec(memory_space=pltpu.HBM)] * 3,
         out_specs=[vmem] * 3,
         scratch_shapes=[
             pltpu.VMEM((len(ROUNDS), tall, width, levels), jnp.float32),
@@ -248,9 +268,16 @@
             pltpu.SemaphoreType.DMA((py,)),
             pltpu.SemaphoreType.DMA((py,)),
         ],
-        compiler_params=pltpu.CompilerParams(collective_id=0, has_side_effects=True),
+        compiler_params=pltpu.CompilerParams(collective_id=0, has_side_effects=True, vmem_limit_bytes=10*2**20),
     )(density, conductance, source)
-    return (density - mean) * scale, density
+    return pl.pallas_call(
+        finish,
+        out_shape=[jax.ShapeDtypeStruct(density.shape, jnp.float32)] * 2,
+        in_specs=[vmem] * 3,
+        out_specs=[pl.BlockSpec(memory_space=pltpu.HBM)] * 2,
+        scratch_shapes=[pltpu.VMEM(density.shape, jnp.float32), pltpu.SemaphoreType.DMA((CHUNKS + 1,))],
+        compiler_params=pltpu.CompilerParams(vmem_limit_bytes=4 * 2**20),
+    )(density, mean, scale)
 
 
 def solution(mesh):

time: 30.8 us -> 28.2 us (0.916)
  other arithmetic: 1.98 us -> 0 us
  local copies, waits for them, and re-layouts: 0.8 us -> 0 us
    mul x1 -> x0, other arithmetic: 1.98 us -> none  [per_device(): return ((density - mean) * scale, density)]
    pallas_call x0 -> x1, Pallas kernels: none -> 1 us  [per_device(): pl.pallas_call(finish, out_shape=[jax.ShapeDtypeStruct(density.shape, jnp...]
    pallas_call x1, Pallas kernels: 27.2 us -> 26.4 us  [per_device(): pl.pallas_call(functools.partial(kernel, py, px), out_shape=[jax.ShapeDty...]
    unnamed x3 -> x0, local copies, waits for them, and re-layouts: 0.8 us -> none
where the time goes in v2:
time: 28.2 us; the launch traced here: 28 us
  Pallas kernels  27.4 us (97%)
  between operations  0.64 us (2%)
    pallas_call x1, Pallas kernels, per_device(): pl.pallas_call(functools.partial(kernel, py, px), out_shape=[jax.ShapeDty...  26.4 us
    pallas_call x1, Pallas kernels, per_device(): pl.pallas_call(finish, out_shape=[jax.ShapeDtypeStruct(density.shape, jnp...  1 us

profile of v2, /device:TPU:0, one launch (start us, length us, event | category | flops | bytes accessed | tf_op | source)
XLA Modules:
  0.0 28.0 jit_solution(17370030513735384021)
XLA Ops:
  0.6 26.4 %shard_map.50 = (f32[32,32,128]{2,1,0:T(8,128)S(1)}, f32[32,128]{1,0:T(8,128)S(1)}, f32[32,128]{1,0:T(8,128)S(1)}) custom-call(f32[32,32,128]{2,1,0:T(8,128)} %field.1, f32[32,32,128]{2,1,0:T(8,128)} %conductance.1, f32[32,32,128]{2,1,0:T(8,128)} %source.1), custom_call_target="tpu_custom_call" | custom-call | tf_op jit(solution)/shard_map/pallas_call | solution.py:255
  27.0 1.0 %shard_map.51 = (f32[32,32,128]{2,1,0:T(8,128)}, f32[32,32,128]{2,1,0:T(8,128)}) custom-call(f32[32,32,128]{2,1,0:T(8,128)S(1)} %get-tuple-element.5.density, f32[32,128]{1,0:T(8,128)S(1)} %get-tuple-element.6.mean, f32[32,128]{1,0:T(8,128)S(1)} %get-tuple-element.7.scale), custom_call_target="tpu_custom_call" | custom-call | tf_op jit(solution)/shard_map/pallas_call | solution.py:273

commit v3 on v2

--- a/solution.py
+++ b/solution.py
@@ -22,7 +22,7 @@
     return (own, size), (own, size)
 
 
-def kernel(py, px, field, conductance, source, density_out, mean_out, scale_out,
+def kernel(py, px, inner, field, conductance, source, density_out, mean_out, scale_out,
            padded, work, coefficients, stats, local_sem, send_sem, recv_sem, stat_send, stat_recv):
     rows, columns, levels = field.shape
     width = columns + 2 * PAD
@@ -36,12 +36,12 @@
             here = here & ((mx > 0) if dx < 0 else (mx < px - 1))
         return here
 
-    inner = (pl.ds(DEEP, rows), pl.ds(PAD, columns))
+    block = (pl.ds(DEEP, rows), pl.ds(PAD, columns))
     loads = []
     for i, (src, dst) in enumerate(
         [(field, padded.at[0]), (conductance, coefficients.at[0]), (source, coefficients.at[1])]
     ):
-        loads.append(pltpu.make_async_copy(src, dst.at[inner], local_sem.at[i]))
+        loads.append(pltpu.make_async_copy(src, dst.at[block], local_sem.at[i]))
         loads[-1].start()
 
     barrier = pltpu.get_barrier_semaphore()
@@ -194,15 +194,21 @@
     squares = lax.fori_loop(0, rows, square, jnp.zeros((columns, levels), jnp.float32), unroll=4)
     stats[0, 0] = local_mean
     stats[0, 1] = squares
-    order = sorted(range(1, py), key=lambda step: -min(step, py - step))
+    outer = py // inner
+    far_first = sorted(
+        ((do, di) for do in range(outer) for di in range(inner) if do or di),
+        key=lambda place: -(min(place[0], outer - place[0]) + min(place[1], inner - place[1])),
+    )
     sums = []
-    for step in order:
+    for do, di in far_first:
+        step = do * inner + di
+        peer = lax.rem(my // inner + do, outer) * inner + lax.rem(lax.rem(my, inner) + di, inner)
         copy = pltpu.make_async_remote_copy(
             src_ref=stats.at[0],
             dst_ref=stats.at[step],
             send_sem=stat_send.at[step],
             recv_sem=stat_recv.at[step],
-            device_id=(lax.rem(my + step, py), mx),
+            device_id=(peer, mx),
             device_id_type=MESH,
         )
         copy.start()
@@ -246,14 +252,14 @@
     whole.wait()
 
 
-def per_device(py, px, density, conductance, source):
+def per_device(py, px, inner, density, conductance, source):
     rows, columns, levels = density.shape
     tall, width = rows + 2 * DEEP, columns + 2 * PAD
     vmem = pl.BlockSpec(memory_space=pltpu.VMEM)
     line = jax.ShapeDtypeStruct((columns, levels), jnp.float32)
     density, conductance, source = (pltpu.with_memory_space_constraint(x, pltpu.HBM) for x in (density, conductance, source))
     density, mean, scale = pl.pallas_call(
-        functools.partial(kernel, py, px),
+        functools.partial(kernel, py, px, inner),
         out_shape=[jax.ShapeDtypeStruct(density.shape, jnp.float32), line, line],
         in_specs=[pl.BlockSpec(memory_space=pltpu.HBM)] * 3,
         out_specs=[vmem] * 3,
@@ -282,7 +288,10 @@
 
 def solution(mesh):
     spec = P("py", "px", None)
+    line = mesh.devices.reshape(mesh.shape["py"], -1)[:, 0] if mesh.axis_names[0] == "py" else []
+    places = [getattr(device, "coords", (0, 0, 0))[2] for device in line]
+    inner = max(1, places.count(places[0])) if places else 1
     return jax.shard_map(
-        functools.partial(per_device, mesh.shape["py"], mesh.shape["px"]),
+        functools.partial(per_device, mesh.shape["py"], mesh.shape["px"], inner),
         mesh=mesh, in_specs=(spec,) * 3, out_specs=(spec,) * 2, check_vma=False,
     )

time: 28.2 us -> 27.9 us (0.989)
  Pallas kernels: 27.4 us -> 27.1 us
    pallas_call x1, Pallas kernels: 26.4 us -> 26.1 us  [per_device(): pl.pallas_call(functools.partial(kernel, py, px, inner), out_shape=[jax.S...]
where the time goes in v3:
time: 27.9 us; the launch traced here: 27.7 us
  Pallas kernels  27.1 us (97%)
  between operations  0.64 us (2%)
    pallas_call x1, Pallas kernels, per_device(): pl.pallas_call(functools.partial(kernel, py, px, inner), out_shape=[jax.S...  26.1 us
    pallas_call x1, Pallas kernels, per_device(): pl.pallas_call(finish, out_shape=[jax.ShapeDtypeStruct(density.shape, jnp...  1 us

profile of v3, /device:TPU:0, one launch (start us, length us, event | category | flops | bytes accessed | tf_op | source)
XLA Modules:
  0.0 27.7 jit_solution(1975476491770030099)
XLA Ops:
  0.6 26.1 %shard_map.50 = (f32[32,32,128]{2,1,0:T(8,128)S(1)}, f32[32,128]{1,0:T(8,128)S(1)}, f32[32,128]{1,0:T(8,128)S(1)}) custom-call(f32[32,32,128]{2,1,0:T(8,128)} %field.1, f32[32,32,128]{2,1,0:T(8,128)} %conductance.1, f32[32,32,128]{2,1,0:T(8,128)} %source.1), custom_call_target="tpu_custom_call" | custom-call | tf_op jit(solution)/shard_map/pallas_call | solution.py:261
  26.7 1.0 %shard_map.51 = (f32[32,32,128]{2,1,0:T(8,128)}, f32[32,32,128]{2,1,0:T(8,128)}) custom-call(f32[32,32,128]{2,1,0:T(8,128)S(1)} %get-tuple-element.5.density, f32[32,128]{1,0:T(8,128)S(1)} %get-tuple-element.6.mean, f32[32,128]{1,0:T(8,128)S(1)} %get-tuple-element.7.scale), custom_call_target="tpu_custom_call" | custom-call | tf_op jit(solution)/shard_map/pallas_call | solution.py:279

commit v4 on v3

--- a/solution.py
+++ b/solution.py
@@ -10,7 +10,7 @@
 ROUNDS = (3, 3)
 DEEP = max(ROUNDS)
 PAD = 4
-DIRECTIONS = [(0, -1), (0, 1), (-1, 0), (1, 0), (-1, -1), (-1, 1), (1, -1), (1, 1)]
+DIRECTIONS = [(-1, -1), (-1, 1), (1, -1), (1, 1), (-1, 0), (1, 0), (0, -1), (0, 1)]
 MESH = pl.DeviceIdType.MESH
 
 
@@ -131,11 +131,11 @@
             sides = flat[pl.ds(at - 1, wide), :] + flat[pl.ds(at + 1, wide), :]
             spread = (above + below) + sides - 4.0 * middle
             later = middle + flat_conductance[pl.ds(at, wide), :] * spread + flat_source[pl.ds(at, wide), :]
-            return middle, below, put(i, later, carry)
+            return middle, below, put(first - DEEP + i, later, carry)
 
         at = first * width + column
         state = (flat[pl.ds(at - width, wide), :], flat[pl.ds(at, wide), :], carry)
-        return lax.fori_loop(0, count, row, state, unroll=2)[2]
+        return lax.fori_loop(0, count, row, state, unroll=min(count, 4))[2]
 
     total = jnp.zeros((columns, levels), jnp.float32)
     waiting = []
@@ -153,37 +153,35 @@
             for copy in loads:
                 copy.wait()
         start(copies)
-        wait_recv(copies)
         waiting.append(copies)
-        old = padded.at[number]
-        for step in range(steps):
-            margin = steps - 1 - step
-            if margin:
-                new = work.at[step % 2]
-                flat_new = new.reshape(tall * width, levels)
-                first = DEEP - margin
-
-                def put(i, later, carry, first=first, flat_new=flat_new):
-                    flat_new[pl.ds((first + i) * width, width), :] = later
+        across = [copy for copy in copies if not copy[0][0]]
+        wait_recv(across)
+        for part in ("inside", "ends"):
+            if part == "ends":
+                wait_recv([copy for copy in copies if copy[0][0]])
+            old = padded.at[number]
+            for step in range(steps):
+                margin = steps - 1 - step
+                if part == "inside":
+                    spans = [(DEEP + step + 1, rows - 2 * (step + 1))]
+                else:
+                    spans = [(DEEP - margin, steps), (DEEP + rows - step - 1, steps)]
+                column, wide, new = PAD, columns, None
+                if margin:
+                    column, wide, new = 0, width, work.at[step]
+                elif number < len(ROUNDS) - 1:
+                    new = padded.at[number + 1]
+
+                def put(i, later, carry, new=new, column=column, wide=wide):
+                    if new is None:
+                        density_out[i] = later
+                        return carry + later
+                    new.reshape(tall * width, levels)[pl.ds((DEEP + i) * width + column, wide), :] = later
                     return carry
 
-                advance(old, first, rows + 2 * margin, 0, width, put, 0)
+                for first, count in spans:
+                    total = advance(old, first, count, column, wide, put, total)
                 old = new
-            elif number < len(ROUNDS) - 1:
-                flat_new = padded.at[number + 1].reshape(tall * width, levels)
-
-                def put(i, later, carry, flat_new=flat_new):
-                    flat_new[pl.ds((DEEP + i) * width + PAD, columns), :] = later
-                    return carry
-
-                advance(old, DEEP, rows, PAD, columns, put, 0)
-            else:
-
-                def put(i, later, carry):
-                    density_out[i] = later
-                    return carry + later
-
-                total = advance(old, DEEP, rows, PAD, columns, put, total)
 
     local_mean = total * (1.0 / rows)
 
@@ -265,7 +263,7 @@
         out_specs=[vmem] * 3,
         scratch_shapes=[
             pltpu.VMEM((len(ROUNDS), tall, width, levels), jnp.float32),
-            pltpu.VMEM((2, tall, width, levels), jnp.float32),
+            pltpu.VMEM((DEEP - 1, tall, width, levels), jnp.float32),
             pltpu.VMEM((2, tall, width, levels), jnp.float32),
             pltpu.VMEM((py, 2, columns, levels), jnp.float32),
             pltpu.SemaphoreType.DMA((3,)),

time: 27.9 us -> 26.3 us (0.943)
  Pallas kernels: 27.1 us -> 25.5 us
    pallas_call x1, Pallas kernels: 26.1 us -> 24.5 us  [per_device(): pl.pallas_call(functools.partial(kernel, py, px, inner), out_shape=[jax.S...]
where the time goes in v4:
time: 26.3 us; the launch traced here: 26.2 us
  Pallas kernels  25.5 us (97%)
  between operations  0.64 us (2%)
    pallas_call x1, Pallas kernels, per_device(): pl.pallas_call(functools.partial(kernel, py, px, inner), out_shape=[jax.S...  24.5 us
    pallas_call x1, Pallas kernels, per_device(): pl.pallas_call(finish, out_shape=[jax.ShapeDtypeStruct(density.shape, jnp...  1 us

profile of v4, /device:TPU:0, one launch (start us, length us, event | category | flops | bytes accessed | tf_op | source)
XLA Modules:
  0.0 26.2 jit_solution(6663899749751910716)
XLA Ops:
  0.6 24.5 %shard_map.50 = (f32[32,32,128]{2,1,0:T(8,128)S(1)}, f32[32,128]{1,0:T(8,128)S(1)}, f32[32,128]{1,0:T(8,128)S(1)}) custom-call(f32[32,32,128]{2,1,0:T(8,128)} %field.1, f32[32,32,128]{2,1,0:T(8,128)} %conductance.1, f32[32,32,128]{2,1,0:T(8,128)} %source.1), custom_call_target="tpu_custom_call" | custom-call | tf_op jit(solution)/shard_map/pallas_call | solution.py:259
  25.2 1.0 %shard_map.51 = (f32[32,32,128]{2,1,0:T(8,128)}, f32[32,32,128]{2,1,0:T(8,128)}) custom-call(f32[32,32,128]{2,1,0:T(8,128)S(1)} %get-tuple-element.5.density, f32[32,128]{1,0:T(8,128)S(1)} %get-tuple-element.6.mean, f32[32,128]{1,0:T(8,128)S(1)} %get-tuple-element.7.scale), custom_call_target="tpu_custom_call" | custom-call | tf_op jit(solution)/shard_map/pallas_call | solution.py:277

commit v5 on v4

--- a/solution.py
+++ b/solution.py
@@ -84,10 +84,11 @@
                 (x_from, x_size), _ = edge(dx, columns, reach, column0)
                 _, (y_to, _) = edge(dy, rows, reach, DEEP)
                 _, (x_to, _) = edge(dx, columns, reach, PAD)
+                both = (slice(None),) * (len(src.shape) - 3)
                 copies.append(
                     pltpu.make_async_remote_copy(
-                        src_ref=src.at[pl.ds(y_from, y_size), pl.ds(x_from, x_size)],
-                        dst_ref=dst.at[pl.ds(y_to, y_size), pl.ds(x_to, x_size)],
+                        src_ref=src.at[both + (pl.ds(y_from, y_size), pl.ds(x_from, x_size))],
+                        dst_ref=dst.at[both + (pl.ds(y_to, y_size), pl.ds(x_to, x_size))],
                         send_sem=send_sem.at[number, a, d],
                         recv_sem=recv_sem.at[number, a, d],
                         device_id=(my + dy, mx + dx),
@@ -143,8 +144,7 @@
         if number == 0:
             arrays = [
                 (padded.at[0], DEEP, PAD, padded.at[0], steps),
-                (coefficients.at[0], DEEP, PAD, coefficients.at[0], DEEP - 1),
-                (coefficients.at[1], DEEP, PAD, coefficients.at[1], DEEP - 1),
+                (coefficients, DEEP, PAD, coefficients, DEEP - 1),
             ]
         else:
             arrays = [(padded.at[number], DEEP, PAD, padded.at[number], steps)]
@@ -156,16 +156,19 @@
         waiting.append(copies)
         across = [copy for copy in copies if not copy[0][0]]
         wait_recv(across)
-        for part in ("inside", "ends"):
-            if part == "ends":
-                wait_recv([copy for copy in copies if copy[0][0]])
+        for part in ("inside", "low", "high"):
+            if part != "inside":
+                sent = 1 if part == "low" else -1
+                wait_recv([copy for copy in copies if copy[0][0] == sent])
             old = padded.at[number]
             for step in range(steps):
                 margin = steps - 1 - step
                 if part == "inside":
                     spans = [(DEEP + step + 1, rows - 2 * (step + 1))]
+                elif part == "low":
+                    spans = [(DEEP - margin, steps)]
                 else:
-                    spans = [(DEEP - margin, steps), (DEEP + rows - step - 1, steps)]
+                    spans = [(DEEP + rows - step - 1, steps)]
                 column, wide, new = PAD, columns, None
                 if margin:
                     column, wide, new = 0, width, work.at[step]
@@ -230,7 +233,7 @@
     for copy in sums:
         copy.wait_send()
 
-CHUNKS = 4
+CHUNKS = 2
 
 
 def finish(density, mean, scale, anomaly_out, density_out, anomaly, sem):

time: 26.3 us -> 26.3 us (level)
  no operation moved by 1% of the time
where the time goes in v5:
time: 26.3 us; the launch traced here: 26.1 us
  Pallas kernels  25.5 us (97%)
  between operations  0.64 us (2%)
    pallas_call x1, Pallas kernels, per_device(): pl.pallas_call(functools.partial(kernel, py, px, inner), out_shape=[jax.S...  24.5 us
    pallas_call x1, Pallas kernels, per_device(): pl.pallas_call(finish, out_shape=[jax.ShapeDtypeStruct(density.shape, jnp...  0.99 us

profile of v5, /device:TPU:0, one launch (start us, length us, event | category | flops | bytes accessed | tf_op | source)
XLA Modules:
  0.0 26.1 jit_solution(8012177322114492861)
XLA Ops:
  0.6 24.5 %shard_map.50 = (f32[32,32,128]{2,1,0:T(8,128)S(1)}, f32[32,128]{1,0:T(8,128)S(1)}, f32[32,128]{1,0:T(8,128)S(1)}) custom-call(f32[32,32,128]{2,1,0:T(8,128)} %field.1, f32[32,32,128]{2,1,0:T(8,128)} %conductance.1, f32[32,32,128]{2,1,0:T(8,128)} %source.1), custom_call_target="tpu_custom_call" | custom-call | tf_op jit(solution)/shard_map/pallas_call | solution.py:262
  25.1 1.0 %shard_map.51 = (f32[32,32,128]{2,1,0:T(8,128)}, f32[32,32,128]{2,1,0:T(8,128)}) custom-call(f32[32,32,128]{2,1,0:T(8,128)S(1)} %get-tuple-element.5.density, f32[32,128]{1,0:T(8,128)S(1)} %get-tuple-element.6.mean, f32[32,128]{1,0:T(8,128)S(1)} %get-tuple-element.7.scale), custom_call_target="tpu_custom_call" | custom-call | tf_op jit(solution)/shard_map/pallas_call | solution.py:280

commit v6 on v4

--- a/solution.py
+++ b/solution.py
@@ -35,14 +35,6 @@
         if dx:
             here = here & ((mx > 0) if dx < 0 else (mx < px - 1))
         return here
-
-    block = (pl.ds(DEEP, rows), pl.ds(PAD, columns))
-    loads = []
-    for i, (src, dst) in enumerate(
-        [(field, padded.at[0]), (conductance, coefficients.at[0]), (source, coefficients.at[1])]
-    ):
-        loads.append(pltpu.make_async_copy(src, dst.at[block], local_sem.at[i]))
-        loads[-1].start()
 
     barrier = pltpu.get_barrier_semaphore()
     expected = jnp.int32(py - 1)
@@ -56,6 +48,14 @@
             @pl.when(there)
             def _():
                 pl.semaphore_signal(barrier, 1, device_id=(my + dy, mx + dx), device_id_type=MESH)
+
+    block = (pl.ds(DEEP, rows), pl.ds(PAD, columns))
+    loads = []
+    for i, (src, dst) in enumerate(
+        [(field, padded.at[0]), (conductance, coefficients.at[0]), (source, coefficients.at[1])]
+    ):
+        loads.append(pltpu.make_async_copy(src, dst.at[block], local_sem.at[i]))
+        loads[-1].start()
 
     holders = [padded.at[r] for r in range(len(ROUNDS))] + [coefficients.at[0], coefficients.at[1]]
     for dim, direction in ((0, -1), (0, 1), (1, -1), (1, 1)):
@@ -195,7 +195,7 @@
     outer = py // inner
     far_first = sorted(
         ((do, di) for do in range(outer) for di in range(inner) if do or di),
-        key=lambda place: -(min(place[0], outer - place[0]) + min(place[1], inner - place[1])),
+        key=lambda place: (-min(place[0], outer - place[0]), -place[1]),
     )
     sums = []
     for do, di in far_first:

time: 26.3 us -> 26.3 us (level)
  no operation moved by 1% of the time
where the time goes in v6:
time: 26.3 us; the launch traced here: 26.2 us
  Pallas kernels  25.5 us (97%)
  between operations  0.64 us (2%)
    pallas_call x1, Pallas kernels, per_device(): pl.pallas_call(functools.partial(kernel, py, px, inner), out_shape=[jax.S...  24.5 us
    pallas_call x1, Pallas kernels, per_device(): pl.pallas_call(finish, out_shape=[jax.ShapeDtypeStruct(density.shape, jnp...  1 us

profile of v6, /device:TPU:0, one launch (start us, length us, event | category | flops | bytes accessed | tf_op | source)
XLA Modules:
  0.0 26.2 jit_solution(11749164071032734326)
XLA Ops:
  0.6 24.5 %shard_map.50 = (f32[32,32,128]{2,1,0:T(8,128)S(1)}, f32[32,128]{1,0:T(8,128)S(1)}, f32[32,128]{1,0:T(8,128)S(1)}) custom-call(f32[32,32,128]{2,1,0:T(8,128)} %field.1, f32[32,32,128]{2,1,0:T(8,128)} %conductance.1, f32[32,32,128]{2,1,0:T(8,128)} %source.1), custom_call_target="tpu_custom_call" | custom-call | tf_op jit(solution)/shard_map/pallas_call | solution.py:259
  25.2 1.0 %shard_map.51 = (f32[32,32,128]{2,1,0:T(8,128)}, f32[32,32,128]{2,1,0:T(8,128)}) custom-call(f32[32,32,128]{2,1,0:T(8,128)S(1)} %get-tuple-element.5.density, f32[32,128]{1,0:T(8,128)S(1)} %get-tuple-element.6.mean, f32[32,128]{1,0:T(8,128)S(1)} %get-tuple-element.7.scale), custom_call_target="tpu_custom_call" | custom-call | tf_op jit(solution)/shard_map/pallas_call | solution.py:277
